TPU v7x, 32 devices: a whole 2x2x4 slice. The times are simulated.
32 devices in a mesh: head: 8 (over z, core), kv: 4 (over y, x).
Axes of the slice: x: 2, y: 2, z: 4, core: 2. Of those that a mesh axis runs over, the one named last changes fastest.
Arguments:
- queries: bfloat16 [2048, 8192], P(('kv', 'head')), may hold values from -6 to 6
- key_rows: bfloat16 [2048, 1024], P(('kv', 'head')), may hold values from -6 to 6
- value_matrix: bfloat16 [2048, 1024], P(('kv', 'head')), may hold values from -6 to 6
- doc_ids: int32 [2048], P(('kv', 'head')), may hold values from 0 to 5, as said below
Outputs:
- attended: bfloat16 [2048, 8192], P(('kv', 'head'))
Inputs may be any that keep to these rules, and one draw needn't show every extreme that they name: doc_ids starts at 0, never falls, and rises by one at the first token of each of the 6 documents; every document starts at an even position and has 2 tokens or more.
All inputs are finite; a program needn't handle non-finite values.
Results may differ from a plain program's by a relative error of at most 0.015.
Values may be sent and summed in bfloat16 or wider, within the bound.
A program may use at most 64 MiB of HBM per device.

v0:
```python
import math
import jax
import jax.numpy as jnp
from jax import lax
from jax.sharding import PartitionSpec as P

QUERY_HEADS = 64
KEY_VALUE_HEADS = 8
HEAD_SIZE = 128
NEG_FILL = -1e30


def repeat_heads(input_matrix, head_repeats):
    row_number = input_matrix.shape[0]
    heads_apart = input_matrix.reshape(row_number, KEY_VALUE_HEADS, 1, HEAD_SIZE)
    expanded_heads = jnp.broadcast_to(
        heads_apart, (row_number, KEY_VALUE_HEADS, head_repeats, HEAD_SIZE)
    )
    return expanded_heads.reshape(row_number, KEY_VALUE_HEADS * head_repeats * HEAD_SIZE)


def block_terms(query_group, query_pos, query_doc, key_block, value_block, key_pos, key_doc):
    key_count = key_block.shape[0]
    key_value_slot = query_group.shape[1]
    key_heads = key_block.reshape(key_count, key_value_slot, HEAD_SIZE)
    value_heads = value_block.reshape(key_count, key_value_slot, HEAD_SIZE)
    scores = jnp.einsum(
        "rkgd,ckd->kgrc", query_group, key_heads, preferred_element_type=jnp.float32
    ) * HEAD_SIZE ** (-0.5)
    allowed = (key_pos[None, :] <= query_pos[:, None]) & (key_doc[None, :] == query_doc[:, None])
    masked = jnp.where(allowed, scores, NEG_FILL)
    row_peak = jnp.max(masked, axis=-1)
    weights = jnp.where(allowed, jnp.exp(masked - row_peak[..., None]), 0.0)
    row_total = jnp.sum(weights, axis=-1)
    weighted = jnp.einsum(
        "kgrc,ckd->kgrd",
        weights.astype(jnp.bfloat16),
        value_heads,
        preferred_element_type=jnp.float32,
    )
    return (row_peak, row_total, weighted)


def attend_block(query_group, query_pos, query_doc, key_block, value_block, key_pos, key_doc):
    return block_terms(query_group, query_pos, query_doc, key_block, value_block, key_pos, key_doc)


def combine_terms(first_terms, second_terms):
    joint_peak = jnp.maximum(first_terms[0], second_terms[0])
    left_factor = jnp.exp(first_terms[0] - joint_peak)
    right_factor = jnp.exp(second_terms[0] - joint_peak)
    joint_total = first_terms[1] * left_factor + second_terms[1] * right_factor
    joint_weighted = (
        first_terms[2] * left_factor[..., None] + second_terms[2] * right_factor[..., None]
    )
    return (joint_peak, joint_total, joint_weighted)


def local(queries, key_rows, value_matrix, doc_ids):
    head_number = lax.axis_size("head")
    head_repeats = max(1, head_number // KEY_VALUE_HEADS)
    key_send = repeat_heads(key_rows, head_repeats)
    value_send = repeat_heads(value_matrix, head_repeats)
    query_block, key_block, value_block = (
        lax.all_to_all(queries, "head", split_axis=1, concat_axis=0, tiled=True),
        lax.all_to_all(key_send, "head", split_axis=1, concat_axis=0, tiled=True),
        lax.all_to_all(value_send, "head", split_axis=1, concat_axis=0, tiled=True),
    )
    block_len = query_block.shape[0]
    doc_global = lax.all_gather(doc_ids, ("kv", "head"), axis=0, tiled=True)
    query_width = query_block.shape[1]
    present_heads = query_width // HEAD_SIZE
    key_value_slot = max(1, present_heads // (QUERY_HEADS // KEY_VALUE_HEADS))
    group_here = present_heads // key_value_slot
    own_first = lax.axis_index("kv") * block_len
    own_pos = own_first + jnp.arange(block_len, dtype=jnp.int32)
    own_doc = jnp.take(doc_global, own_pos)
    query_group = query_block.reshape(block_len, key_value_slot, group_here, HEAD_SIZE)
    term_shape = (key_value_slot, group_here, block_len)
    initial = (
        jnp.full(term_shape, NEG_FILL, jnp.float32),
        jnp.zeros(term_shape, jnp.float32),
        jnp.zeros(term_shape + (HEAD_SIZE,), jnp.float32),
    )
    key_piece = lax.all_gather(key_block, "kv", axis=0, tiled=True)
    value_piece = lax.all_gather(value_block, "kv", axis=0, tiled=True)
    piece_rows = key_piece.shape[0]
    step_rows = math.gcd(piece_rows, 1024)

    def one_step(step_index, inner):
        local_first = step_index * step_rows
        keys_now = lax.dynamic_slice_in_dim(key_piece, local_first, step_rows, 0)
        values_now = lax.dynamic_slice_in_dim(value_piece, local_first, step_rows, 0)
        key_pos = local_first + jnp.arange(step_rows, dtype=jnp.int32)
        key_doc = jnp.take(doc_global, key_pos)
        return combine_terms(
            inner,
            attend_block(query_group, own_pos, own_doc, keys_now, values_now, key_pos, key_doc),
        )

    folded = lax.fori_loop(0, piece_rows // step_rows, one_step, initial)
    result = (
        (folded[2] / folded[1][..., None]).transpose(2, 0, 1, 3).reshape(block_len, query_width)
    )
    result = result.astype(jnp.bfloat16)
    return lax.all_to_all(result, "head", split_axis=0, concat_axis=1, tiled=True)


def solution(mesh):
    return jax.shard_map(
        local,
        mesh=mesh,
        in_specs=(
            P(("kv", "head"), None),
            P(("kv", "head"), None),
            P(("kv", "head"), None),
            P(("kv", "head")),
        ),
        out_specs=P(("kv", "head"), None),
        check_vma=False,
    )
```

profile of v0, /device:TPU:0, one launch (start us, length us, event | category | flops | bytes accessed | tf_op | source)
XLA Modules:
  0.0 176.7 jit_solution(10033229204570758715)
XLA Ops:
  0.0 0.0 copy-start
  0.0 0.9 copy-done
  0.9 0.7 copy_bitcast_fusion.2
  1.6 6.4 %all-to-all-start = ((bf16[64,8,128]{2,0,1:T(8,128)(2,1)}), bf16[64,8,128]{2,0,1:T(8,128)(2,1)S(1)}, u32[]{:S(2)}, u32[]{:S(2)}) async-start(bf16[64,8,128]{2,0,1:T(8,128)(2,1)} %copy_bitcast_fusion.2), calls=%async_computation | async-start | bytes 262144 | tf_op jit(solution)/shard_map/all_to_all | solution.py:66
  7.9 1.6 copy_bitcast_fusion.1
  9.5 5.2 %all-to-all-done = bf16[64,8,128]{2,0,1:T(8,128)(2,1)S(1)} async-done(((bf16[64,8,128]{2,0,1:T(8,128)(2,1)}), bf16[64,8,128]{2,0,1:T(8,128)(2,1)S(1)}, u32[]{:S(2)}, u32[]{:S(2)}) %all-to-all-start) | async-done | bytes 131104 | tf_op jit(solution)/shard_map/all_to_all | solution.py:66
  14.7 3.4 %all-to-all-start.2 = ((bf16[64,8,128]{2,0,1:T(8,128)(2,1)}), bf16[64,8,128]{2,0,1:T(8,128)(2,1)S(1)}, u32[]{:S(2)}, u32[]{:S(2)}) async-start(bf16[64,8,128]{2,0,1:T(8,128)(2,1)} %copy_bitcast_fusion.1), calls=%async_computation.2 | async-start | bytes 262144 | tf_op jit(solution)/shard_map/all_to_all | solution.py:67
  18.1 2.3 %copy.30 = bf16[8,8,8,1024]{3,2,0,1:T(8,128)(2,1)} copy(bf16[8,8,8,1024]{3,2,1,0:T(8,128)(2,1)} %bitcast.121) | data formatting | bytes 2097152 | tf_op jit(solution)/shard_map/all_to_all | solution.py:65
  20.4 4.4 %all-to-all-done.2 = bf16[64,8,128]{2,0,1:T(8,128)(2,1)S(1)} async-done(((bf16[64,8,128]{2,0,1:T(8,128)(2,1)}), bf16[64,8,128]{2,0,1:T(8,128)(2,1)S(1)}, u32[]{:S(2)}, u32[]{:S(2)}) %all-to-all-start.2) | async-done | bytes 131104 | tf_op jit(solution)/shard_map/all_to_all | solution.py:67
  24.8 3.6 %all-to-all-start.1 = ((bf16[64,8,1024]{2,0,1:T(8,128)(2,1)}), bf16[64,8,1024]{2,0,1:T(8,128)(2,1)S(1)}, u32[]{:S(2)}, u32[]{:S(2)}) async-start(bf16[64,8,1024]{2,0,1:T(8,128)(2,1)} %bitcast.93), calls=%async_computation.1 | async-start | bytes 2097152 | tf_op jit(solution)/shard_map/all_to_all | solution.py:65
  28.4 1.3 dynamic-slice
  30.4 0.9 dynamic-update-slice
  31.2 43.9 %all-reduce = s32[2048]{0:T(1024)S(1)} all-reduce(s32[2048]{0:T(1024)S(1)} %dynamic-update-slice), channel_id=1, replica_groups=mesh['head'=8,'kv'=4] {'kv','head'}, use_global_device_ids=true, to_apply=%add | all-reduce | flops 2048 | bytes 16384
  75.2 3.1 %gather_fusion.1 = s32[512]{0:T(512)S(1)} fusion(s32[2048]{0:T(1024)S(1)} %all-reduce, s32[1024]{0:T(1024)S(1)} %pad_clamp_fusion), kind=kCustom, calls=%fused_computation.1 | custom fusion | bytes 6144 | tf_op jit(solution)/shard_map/jit(_take)/gather | solution.py:77
  78.3 11.6 %all_gather.11 = bf16[2048,128]{1,0:T(8,128)(2,1)S(1)} all-gather(bf16[512,128]{1,0:T(8,128)(2,1)S(1)} %bitcast.124), channel_id=1, replica_groups=mesh['head'=8,'kv'=4] {'kv'}, dimensions={0}, use_global_device_ids=true | all-gather | bytes 655360 | tf_op jit(solution)/shard_map/all_gather | solution.py:86
  89.9 9.0 %all_gather.10 = bf16[2048,128]{1,0:T(8,128)(2,1)S(1)} all-gather(bf16[512,128]{1,0:T(8,128)(2,1)S(1)} %bitcast.123), channel_id=1, replica_groups=mesh['head'=8,'kv'=4] {'kv'}, dimensions={0}, use_global_device_ids=true | all-gather | bytes 655360 | tf_op jit(solution)/shard_map/all_gather | solution.py:85
  98.9 0.0 all-to-all-done.1
  98.9 0.3 copy.26
  99.2 0.1 copy.18
  99.3 43.2 %while.18 = (s32[]{:T(128)}, f32[1,8,512]{2,1,0:T(8,128)S(1)}, f32[1,8,512]{2,1,0:T(8,128)S(1)}, f32[1,8,512,128]{3,2,1,0:T(8,128)}, s32[2048]{0:T(1024)S(1)}, /...) while((s32[]{:T(128)}, f32[1,8,512]{2,1,0:T(8,128)S(1)}, ...), condition=%wide.region_3.4_spmd.clone, body=%wide.region_0.3_spmd.clone.sunk | while | flops 2205726208 | bytes 75335952 | solution.py:101
  99.4 6.2 %gather_fusion = s32[1024]{0:T(1024)S(1)} fusion(s32[2048]{0:T(1024)S(1)} %get-tuple-element.370, s32[1024]{0:T(1024)S(1)} %broadcast_clamp_fusion.2), kind=kCustom, calls=%fused_computation.clone.clone.1 | custom fusion | bytes 12288 | tf_op jit(solution)/shard_map/while/body/eval_jaxpr/jit(_take)/gather | solution.py:95
  105.6 0.8 compare_and_fusion.2
  106.4 2.9 %fusion.41 = (f32[8,512]{1,0:T(8,128)S(1)}, f32[1024,512,8]{1,0,2:T(8,128)S(1)}) fusion(pred[512,1024]{0,1:T(8,128)(4,1)S(1)} %compare_and_fusion.2, bf16[512,1,8,128]{3,0,2,1:T(8,128)(2,1)S(1)} %get-tuple-element.373, bf16[2048,128]{1,0:T(8,128)(2,1)S(1)} %get-tuple-element.372, s32[]{:T(128)S(6)} %select_n.145), kind=kOutput, calls=%fused_computation.5.clone.1 | convolution fusion | flops 1086320640 | bytes 18628612 | tf_op jit(solution)/shard_map/while/body/eval_jaxpr/rkgd,ckd->kgrc/dot_general | solution.py:27
  109.3 0.0 copy-start.1
  109.3 4.0 %fusion.43 = f32[8,512]{1,0:T(8,128)S(1)} fusion(f32[1024,512,8]{1,0,2:T(8,128)S(1)} %get-tuple-element.334, f32[8,512]{1,0:T(8,128)S(1)} %get-tuple-element.332, pred[512,1024]{0,1:T(8,128)(4,1)S(1)} %compare_and_fusion.2), kind=kLoop, calls=%fused_computation.7.clone.1 | loop fusion | flops 20967424 | bytes 17334272 | tf_op jit(solution)/shard_map/while/body/eval_jaxpr/reduce_sum | solution.py:34
  113.4 0.0 copy-done.1
  113.4 6.1 %bitcast_add_fusion.2 = f32[1,8,512,128]{3,2,1,0:T(8,128)S(1)} fusion(f32[1,8,512,128]{3,2,1,0:T(8,128)S(1)} %copy-done.1, f32[1024,512,8]{1,0,2:T(8,128)S(1)} %get-tuple-element.334, f32[8,512]{1,0:T(8,128)S(1)} %get-tuple-element.332, pred[512,1024]{0,1:T(8,128)(4,1)S(1)} %compare_and_fusion.2, f32[8,512]{1,0:T(8,128)S(1)} %get-tuple-element.336, ...), kind=kOutput, calls=%fused_computation.11.clone.1 | convolution fusion | flops 1096810496 | bytes 21807108 | tf_op jit(solution)/shard_map/while/body/eval_jaxpr/kgrc,ckd->kgrd/dot_general | solution.py:35
  119.6 0.0 copy-start.2
  119.6 1.3 copy-done.2
  120.9 6.2 %gather_fusion = s32[1024]{0:T(1024)S(1)} fusion(s32[2048]{0:T(1024)S(1)} %get-tuple-element.370, s32[1024]{0:T(1024)S(1)} %broadcast_clamp_fusion.2), kind=kCustom, calls=%fused_computation.clone.clone.1 | custom fusion | bytes 12288 | tf_op jit(solution)/shard_map/while/body/eval_jaxpr/jit(_take)/gather | solution.py:95
  127.1 0.8 compare_and_fusion.2
  128.0 2.9 %fusion.41 = (f32[8,512]{1,0:T(8,128)S(1)}, f32[1024,512,8]{1,0,2:T(8,128)S(1)}) fusion(pred[512,1024]{0,1:T(8,128)(4,1)S(1)} %compare_and_fusion.2, bf16[512,1,8,128]{3,0,2,1:T(8,128)(2,1)S(1)} %get-tuple-element.373, bf16[2048,128]{1,0:T(8,128)(2,1)S(1)} %get-tuple-element.372, s32[]{:T(128)S(6)} %select_n.145), kind=kOutput, calls=%fused_computation.5.clone.1 | convolution fusion | flops 1086320640 | bytes 18628612 | tf_op jit(solution)/shard_map/while/body/eval_jaxpr/rkgd,ckd->kgrc/dot_general | solution.py:27
  130.9 0.0 copy-start.1
  130.9 4.0 %fusion.43 = f32[8,512]{1,0:T(8,128)S(1)} fusion(f32[1024,512,8]{1,0,2:T(8,128)S(1)} %get-tuple-element.334, f32[8,512]{1,0:T(8,128)S(1)} %get-tuple-element.332, pred[512,1024]{0,1:T(8,128)(4,1)S(1)} %compare_and_fusion.2), kind=kLoop, calls=%fused_computation.7.clone.1 | loop fusion | flops 20967424 | bytes 17334272 | tf_op jit(solution)/shard_map/while/body/eval_jaxpr/reduce_sum | solution.py:34
  135.0 0.0 copy-done.1
  135.0 6.1 %bitcast_add_fusion.2 = f32[1,8,512,128]{3,2,1,0:T(8,128)S(1)} fusion(f32[1,8,512,128]{3,2,1,0:T(8,128)S(1)} %copy-done.1, f32[1024,512,8]{1,0,2:T(8,128)S(1)} %get-tuple-element.334, f32[8,512]{1,0:T(8,128)S(1)} %get-tuple-element.332, pred[512,1024]{0,1:T(8,128)(4,1)S(1)} %compare_and_fusion.2, f32[8,512]{1,0:T(8,128)S(1)} %get-tuple-element.336, ...), kind=kOutput, calls=%fused_computation.11.clone.1 | convolution fusion | flops 1096810496 | bytes 21807108 | tf_op jit(solution)/shard_map/while/body/eval_jaxpr/kgrc,ckd->kgrd/dot_general | solution.py:35
  141.1 0.0 copy-start.2
  141.2 1.3 copy-done.2
  142.5 2.0 %fusion.26 = bf16[512,1,8,128]{3,0,2,1:T(8,128)(2,1)S(1)} fusion(f32[1,8,512,128]{3,2,1,0:T(8,128)} %get-tuple-element.175, f32[8,512]{1,0:T(8,128)S(1)} %bitcast.122), kind=kLoop, calls=%fused_computation.42 | loop fusion | flops 1048576 | bytes 3162112 | tf_op jit(solution)/shard_map/convert_element_type | solution.py:105
  144.4 0.7 copy.19
  145.1 0.5 convert_element_type.19
  145.6 30.0 %all_to_all.70 = bf16[8,64,1024]{2,1,0:T(8,128)(2,1)S(1)} all-to-all(bf16[8,64,1024]{2,1,0:T(8,128)(2,1)S(1)} %convert_element_type.19), channel_id=1, replica_groups=mesh['head'=8,'kv'=4] {'head'}, dimensions={0} | all-to-all | bytes 2097152 | tf_op jit(solution)/shard_map/all_to_all | solution.py:106
  175.6 1.1 copy.25
  (21 shorter events, 0.2 us)
Async XLA Ops:
  0.0 0.9 copy-start
  1.6 13.1 %all-to-all-start = ((bf16[64,8,128]{2,0,1:T(8,128)(2,1)}), bf16[64,8,128]{2,0,1:T(8,128)(2,1)S(1)}, u32[]{:S(2)}, u32[]{:S(2)}) async-start(bf16[64,8,128]{2,0,1:T(8,128)(2,1)} %copy_bitcast_fusion.2), calls=%async_computation | async-start | bytes 262144 | tf_op jit(solution)/shard_map/all_to_all | solution.py:66
  14.7 10.1 %all-to-all-start.2 = ((bf16[64,8,128]{2,0,1:T(8,128)(2,1)}), bf16[64,8,128]{2,0,1:T(8,128)(2,1)S(1)}, u32[]{:S(2)}, u32[]{:S(2)}) async-start(bf16[64,8,128]{2,0,1:T(8,128)(2,1)} %copy_bitcast_fusion.1), calls=%async_computation.2 | async-start | bytes 262144 | tf_op jit(solution)/shard_map/all_to_all | solution.py:67
  24.8 74.1 %all-to-all-start.1 = ((bf16[64,8,1024]{2,0,1:T(8,128)(2,1)}), bf16[64,8,1024]{2,0,1:T(8,128)(2,1)S(1)}, u32[]{:S(2)}, u32[]{:S(2)}) async-start(bf16[64,8,1024]{2,0,1:T(8,128)(2,1)} %bitcast.93), calls=%async_computation.1 | async-start | bytes 2097152 | tf_op jit(solution)/shard_map/all_to_all | solution.py:65
  109.3 4.1 %copy-start.1 = (f32[1,8,512,128]{3,2,1,0:T(8,128)S(1)}, f32[1,8,512,128]{3,2,1,0:T(8,128)}, u32[]{:S(2)}) copy-start(f32[1,8,512,128]{3,2,1,0:T(8,128)} %get-tuple-element.355) | copy-start | bytes 6291460 | tf_op jit(solution)/shard_map/while
  119.6 1.3 copy-start.2
  130.9 4.1 %copy-start.1 = (f32[1,8,512,128]{3,2,1,0:T(8,128)S(1)}, f32[1,8,512,128]{3,2,1,0:T(8,128)}, u32[]{:S(2)}) copy-start(f32[1,8,512,128]{3,2,1,0:T(8,128)} %get-tuple-element.355) | copy-start | bytes 6291460 | tf_op jit(solution)/shard_map/while
  141.1 1.3 copy-start.2
where the time goes:
time: 177 us
  blocking collectives  94.4 us (53%)
  local copies, waits for them, and re-layouts  28.4 us (16%)
  matrix products  18.1 us (10%)
  starting transfers between devices  13.3 us (8%)
  other arithmetic  11.8 us (7%)
  waiting for transfers between devices  9.58 us (5%)
    unnamed x1, blocking collectives  43.9 us
    all_to_all x1, blocking collectives, local(): lax.all_to_all(result, 'head', split_axis=0, concat_axis=1, tiled=True)  30 us
    gather x2, local copies, waits for them, and re-layouts, one_step(): key_doc = jnp.take(doc_global, key_pos)  12.3 us
    dot_general x2, matrix products, block_terms(): jnp.einsum('kgrc,ckd->kgrd', weights.astype(jnp.bfloat16), value_heads, p...  12.3 us
    all_gather x1, blocking collectives, local(): value_piece = lax.all_gather(value_block, 'kv', axis=0, tiled=True)  11.6 us
    all_gather x1, blocking collectives, local(): key_piece = lax.all_gather(key_block, 'kv', axis=0, tiled=True)  9 us
    reduce_sum x2, other arithmetic, block_terms(): row_total = jnp.sum(weights, axis=-1)  8.05 us
    all_to_all x1, starting transfers between devices, local(): lax.all_to_all(key_send, 'head', split_axis=1, concat_axis=0, tiled=True)  6.35 us
  transfers between devices with their start and end apart: 3, of which 2 were waited for; matrix products, arithmetic and copies ran while one was open for 5% of the time, Pallas kernels for 0%

commit v1 on v0

--- a/solution.py
+++ b/solution.py
@@ -83,7 +83,12 @@
         jnp.zeros(term_shape + (HEAD_SIZE,), jnp.float32),
     )
     key_piece = lax.all_gather(key_block, "kv", axis=0, tiled=True)
-    value_piece = lax.all_gather(value_block, "kv", axis=0, tiled=True)
+    ring = [value_block]
+    for hop in range(3):
+        ring.append(lax.ppermute(ring[-1], "kv", [(dev, (dev + 1) % 4) for dev in range(4)]))
+    value_piece = jnp.roll(
+        jnp.concatenate(ring[::-1], axis=0), (lax.axis_index("kv") + 1) * ring[0].shape[0], axis=0
+    )
     piece_rows = key_piece.shape[0]
     step_rows = math.gcd(piece_rows, 1024)
 

time: 177 us -> 170 us (0.960)
  blocking collectives: 94.4 us -> 83 us
  starting transfers between devices: 13.3 us -> 18.7 us
    all_gather x1 -> x0, blocking collectives: 11.6 us -> none  [local(): value_piece = lax.all_gather(value_block, 'kv', axis=0, tiled=True)]
    ppermute x0 -> x3, starting transfers between devices: none -> 5.41 us  [local(): lax.ppermute(ring[-1], 'kv', [(dev, (dev + 1) % 4) for dev in range(4)])]
    all_to_all x1, starting transfers between devices: 6.35 us -> 3.37 us  [local(): lax.all_to_all(key_send, 'head', split_axis=1, concat_axis=0, tiled=True)]
    all_to_all x1, starting transfers between devices: 3.37 us -> 6.35 us  [local(): lax.all_to_all(value_send, 'head', split_axis=1, concat_axis=0, tiled=True)]
    all_to_all x1, waiting for transfers between devices: 5.18 us -> 2.86 us  [local(): lax.all_to_all(key_send, 'head', split_axis=1, concat_axis=0, tiled=True)]
    unnamed x7 -> x14, local copies, waits for them, and re-layouts: 3.49 us -> 3.62 us
  transfers between devices with their start and end apart: 3 -> 6, of which waited for: 2 -> 2; matrix products, arithmetic and copies ran while one was open for 5% -> 6% of each run, Pallas kernels for 0% -> 0%
where the time goes in v1:
time: 170 us
  blocking collectives  83 us (49%)
  local copies, waits for them, and re-layouts  28.6 us (17%)
  starting transfers between devices  18.7 us (11%)
  matrix products  18.3 us (11%)
  other arithmetic  11.8 us (7%)
  waiting for transfers between devices  8.04 us (5%)
    unnamed x1, blocking collectives  42.4 us
    all_to_all x1, blocking collectives, local(): lax.all_to_all(result, 'head', split_axis=0, concat_axis=1, tiled=True)  30 us
    dot_general x2, matrix products, block_terms(): jnp.einsum('kgrc,ckd->kgrd', weights.astype(jnp.bfloat16), value_heads, p...  12.5 us
    gather x2, local copies, waits for them, and re-layouts, one_step(): key_doc = jnp.take(doc_global, key_pos)  12.3 us
    all_gather x1, blocking collectives, local(): key_piece = lax.all_gather(key_block, 'kv', axis=0, tiled=True)  10.7 us
    reduce_sum x2, other arithmetic, block_terms(): row_total = jnp.sum(weights, axis=-1)  8.05 us
    all_to_all x1, starting transfers between devices, local(): lax.all_to_all(value_send, 'head', split_axis=1, concat_axis=0, tiled=True)  6.35 us
    dot_general x2, matrix products, block_terms(): jnp.einsum('rkgd,ckd->kgrc', query_group, key_heads, preferred_element_ty...  5.86 us
  transfers between devices with their start and end apart: 6, of which 2 were waited for; matrix products, arithmetic and copies ran while one was open for 6% of the time, Pallas kernels for 0%

profile of v1, /device:TPU:0, one launch (start us, length us, event | category | flops | bytes accessed | tf_op | source)
XLA Modules:
  0.0 169.8 jit_solution(5055893882364015732)
XLA Ops:
  0.0 0.0 copy-start
  0.0 0.9 copy-done
  0.9 0.7 copy_bitcast_fusion.1
  1.6 6.4 %all-to-all-start.2 = ((bf16[64,8,128]{2,0,1:T(8,128)(2,1)}), bf16[64,8,128]{2,0,1:T(8,128)(2,1)S(1)}, u32[]{:S(2)}, u32[]{:S(2)}) async-start(bf16[64,8,128]{2,0,1:T(8,128)(2,1)} %copy_bitcast_fusion.1), calls=%async_computation.2 | async-start | bytes 262144 | tf_op jit(solution)/shard_map/all_to_all | solution.py:67
  7.9 1.6 copy_bitcast_fusion.2
  9.5 5.2 %all-to-all-done.2 = bf16[64,8,128]{2,0,1:T(8,128)(2,1)S(1)} async-done(((bf16[64,8,128]{2,0,1:T(8,128)(2,1)}), bf16[64,8,128]{2,0,1:T(8,128)(2,1)S(1)}, u32[]{:S(2)}, u32[]{:S(2)}) %all-to-all-start.2) | async-done | bytes 131104 | tf_op jit(solution)/shard_map/all_to_all | solution.py:67
  14.7 3.4 %all-to-all-start = ((bf16[64,8,128]{2,0,1:T(8,128)(2,1)}), bf16[64,8,128]{2,0,1:T(8,128)(2,1)S(1)}, u32[]{:S(2)}, u32[]{:S(2)}) async-start(bf16[64,8,128]{2,0,1:T(8,128)(2,1)} %copy_bitcast_fusion.2), calls=%async_computation | async-start | bytes 262144 | tf_op jit(solution)/shard_map/all_to_all | solution.py:66
  18.1 1.5 collective-permute-start
  19.6 2.3 %copy.30 = bf16[8,8,8,1024]{3,2,0,1:T(8,128)(2,1)} copy(bf16[8,8,8,1024]{3,2,1,0:T(8,128)(2,1)} %bitcast.124) | data formatting | bytes 2097152 | tf_op jit(solution)/shard_map/all_to_all | solution.py:65
  21.9 2.9 %all-to-all-done = bf16[64,8,128]{2,0,1:T(8,128)(2,1)S(1)} async-done(((bf16[64,8,128]{2,0,1:T(8,128)(2,1)}), bf16[64,8,128]{2,0,1:T(8,128)(2,1)S(1)}, u32[]{:S(2)}, u32[]{:S(2)}) %all-to-all-start) | async-done | bytes 131104 | tf_op jit(solution)/shard_map/all_to_all | solution.py:66
  24.8 3.6 %all-to-all-start.1 = ((bf16[64,8,1024]{2,0,1:T(8,128)(2,1)}), bf16[64,8,1024]{2,0,1:T(8,128)(2,1)S(1)}, u32[]{:S(2)}, u32[]{:S(2)}) async-start(bf16[64,8,1024]{2,0,1:T(8,128)(2,1)} %bitcast.93), calls=%async_computation.1 | async-start | bytes 2097152 | tf_op jit(solution)/shard_map/all_to_all | solution.py:65
  28.3 0.0 collective-permute-done
  28.3 1.5 collective-permute-start.1
  29.9 1.3 dynamic-slice
  31.9 0.9 dynamic-update-slice
  32.8 42.4 %all-reduce = s32[2048]{0:T(1024)S(1)} all-reduce(s32[2048]{0:T(1024)S(1)} %dynamic-update-slice), channel_id=1, replica_groups=mesh['head'=8,'kv'=4] {'kv','head'}, use_global_device_ids=true, to_apply=%add | all-reduce | flops 2048 | bytes 16384
  75.1 3.1 %gather_fusion.1 = s32[512]{0:T(512)S(1)} fusion(s32[2048]{0:T(1024)S(1)} %all-reduce, s32[1024]{0:T(1024)S(1)} %pad_clamp_fusion), kind=kCustom, calls=%fused_computation.1 | custom fusion | bytes 6144 | tf_op jit(solution)/shard_map/jit(_take)/gather | solution.py:77
  78.3 0.0 collective-permute-done.1
  78.3 2.3 %collective-permute-start.2 = (bf16[512,128]{1,0:T(8,128)(2,1)S(1)}, bf16[512,128]{1,0:T(8,128)(2,1)S(1)}, u32[]{:S(2)}, u32[]{:S(2)}) collective-permute-start(bf16[512,128]{1,0:T(8,128)(2,1)S(1)} %collective-permute-done.1), channel_id=1, source_target_pairs={{0,1},{1,2},{2,3},{3,0},{4,5},{5,6},{6,7},{7,4},{8,9},{9,10},{10,1... | collective-permute-start | bytes 393224 | tf_op jit(solution)/shard_map/ppermute | solution.py:88
  80.6 10.7 %all_gather.7 = bf16[2048,128]{1,0:T(8,128)(2,1)S(1)} all-gather(bf16[512,128]{1,0:T(8,128)(2,1)S(1)} %bitcast.126), channel_id=1, replica_groups=mesh['head'=8,'kv'=4] {'kv'}, dimensions={0}, use_global_device_ids=true | all-gather | bytes 655360 | tf_op jit(solution)/shard_map/all_gather | solution.py:85
  91.3 0.0 collective-permute-done.2
  91.6 0.0 all-to-all-done.1
  91.6 0.3 copy.26
  91.9 0.1 copy.18
  92.0 43.6 %while.18 = (s32[]{:T(128)}, f32[1,8,512]{2,1,0:T(8,128)S(1)}, f32[1,8,512]{2,1,0:T(8,128)S(1)}, f32[1,8,512,128]{3,2,1,0:T(8,128)}, s32[2048]{0:T(1024)S(1)}, /...) while((s32[]{:T(128)}, f32[1,8,512]{2,1,0:T(8,128)S(1)}, ...), condition=%wide.region_3.4_spmd.clone, body=%wide.region_0.3_spmd.clone.sunk | while | flops 2205726208 | bytes 75335952 | solution.py:106
  92.3 6.2 %gather_fusion = s32[1024]{0:T(1024)S(1)} fusion(s32[2048]{0:T(1024)S(1)} %get-tuple-element.370, s32[1024]{0:T(1024)S(1)} %broadcast_clamp_fusion.2), kind=kCustom, calls=%fused_computation.clone.clone.1 | custom fusion | bytes 12288 | tf_op jit(solution)/shard_map/while/body/eval_jaxpr/jit(_take)/gather | solution.py:100
  98.5 0.8 compare_and_fusion.2
  99.3 2.9 %fusion.41 = (f32[8,512]{1,0:T(8,128)S(1)}, f32[1024,512,8]{1,0,2:T(8,128)S(1)}) fusion(pred[512,1024]{0,1:T(8,128)(4,1)S(1)} %compare_and_fusion.2, bf16[512,1,8,128]{3,0,2,1:T(8,128)(2,1)S(1)} %get-tuple-element.373, bf16[2048,128]{1,0:T(8,128)(2,1)S(1)} %get-tuple-element.372, s32[]{:T(128)S(6)} %select_n.160), kind=kOutput, calls=%fused_computation.5.clone.1 | convolution fusion | flops 1086320640 | bytes 18628612 | tf_op jit(solution)/shard_map/while/body/eval_jaxpr/rkgd,ckd->kgrc/dot_general | solution.py:27
  102.2 0.0 copy-start.1
  102.3 4.0 %fusion.43 = f32[8,512]{1,0:T(8,128)S(1)} fusion(f32[1024,512,8]{1,0,2:T(8,128)S(1)} %get-tuple-element.334, f32[8,512]{1,0:T(8,128)S(1)} %get-tuple-element.332, pred[512,1024]{0,1:T(8,128)(4,1)S(1)} %compare_and_fusion.2), kind=kLoop, calls=%fused_computation.7.clone.1 | loop fusion | flops 20967424 | bytes 17334272 | tf_op jit(solution)/shard_map/while/body/eval_jaxpr/reduce_sum | solution.py:34
  106.3 0.0 copy-done.1
  106.4 6.2 %bitcast_add_fusion.2 = f32[1,8,512,128]{3,2,1,0:T(8,128)S(1)} fusion(f32[1,8,512,128]{3,2,1,0:T(8,128)S(1)} %copy-done.1, f32[1024,512,8]{1,0,2:T(8,128)S(1)} %get-tuple-element.334, f32[8,512]{1,0:T(8,128)S(1)} %get-tuple-element.332, pred[512,1024]{0,1:T(8,128)(4,1)S(1)} %compare_and_fusion.2, f32[8,512]{1,0:T(8,128)S(1)} %get-tuple-element.336, ...), kind=kOutput, calls=%fused_computation.11.clone.1 | convolution fusion | flops 1096810496 | bytes 21807108 | tf_op jit(solution)/shard_map/while/body/eval_jaxpr/kgrc,ckd->kgrd/dot_general | solution.py:35
  112.6 0.0 copy-start.2
  112.6 1.3 copy-done.2
  114.0 6.2 %gather_fusion = s32[1024]{0:T(1024)S(1)} fusion(s32[2048]{0:T(1024)S(1)} %get-tuple-element.370, s32[1024]{0:T(1024)S(1)} %broadcast_clamp_fusion.2), kind=kCustom, calls=%fused_computation.clone.clone.1 | custom fusion | bytes 12288 | tf_op jit(solution)/shard_map/while/body/eval_jaxpr/jit(_take)/gather | solution.py:100
  120.2 0.8 compare_and_fusion.2
  121.0 2.9 %fusion.41 = (f32[8,512]{1,0:T(8,128)S(1)}, f32[1024,512,8]{1,0,2:T(8,128)S(1)}) fusion(pred[512,1024]{0,1:T(8,128)(4,1)S(1)} %compare_and_fusion.2, bf16[512,1,8,128]{3,0,2,1:T(8,128)(2,1)S(1)} %get-tuple-element.373, bf16[2048,128]{1,0:T(8,128)(2,1)S(1)} %get-tuple-element.372, s32[]{:T(128)S(6)} %select_n.160), kind=kOutput, calls=%fused_computation.5.clone.1 | convolution fusion | flops 1086320640 | bytes 18628612 | tf_op jit(solution)/shard_map/while/body/eval_jaxpr/rkgd,ckd->kgrc/dot_general | solution.py:27
  124.0 0.0 copy-start.1
  124.0 4.0 %fusion.43 = f32[8,512]{1,0:T(8,128)S(1)} fusion(f32[1024,512,8]{1,0,2:T(8,128)S(1)} %get-tuple-element.334, f32[8,512]{1,0:T(8,128)S(1)} %get-tuple-element.332, pred[512,1024]{0,1:T(8,128)(4,1)S(1)} %compare_and_fusion.2), kind=kLoop, calls=%fused_computation.7.clone.1 | loop fusion | flops 20967424 | bytes 17334272 | tf_op jit(solution)/shard_map/while/body/eval_jaxpr/reduce_sum | solution.py:34
  128.1 0.0 copy-done.1
  128.1 6.2 %bitcast_add_fusion.2 = f32[1,8,512,128]{3,2,1,0:T(8,128)S(1)} fusion(f32[1,8,512,128]{3,2,1,0:T(8,128)S(1)} %copy-done.1, f32[1024,512,8]{1,0,2:T(8,128)S(1)} %get-tuple-element.334, f32[8,512]{1,0:T(8,128)S(1)} %get-tuple-element.332, pred[512,1024]{0,1:T(8,128)(4,1)S(1)} %compare_and_fusion.2, f32[8,512]{1,0:T(8,128)S(1)} %get-tuple-element.336, ...), kind=kOutput, calls=%fused_computation.11.clone.1 | convolution fusion | flops 1096810496 | bytes 21807108 | tf_op jit(solution)/shard_map/while/body/eval_jaxpr/kgrc,ckd->kgrd/dot_general | solution.py:35
  134.3 0.0 copy-start.2
  134.3 1.3 copy-done.2
  135.7 2.0 %fusion.26 = bf16[512,1,8,128]{3,0,2,1:T(8,128)(2,1)S(1)} fusion(f32[1,8,512,128]{3,2,1,0:T(8,128)} %get-tuple-element.175, f32[8,512]{1,0:T(8,128)S(1)} %bitcast.125), kind=kLoop, calls=%fused_computation.42 | loop fusion | flops 1048576 | bytes 3162112 | tf_op jit(solution)/shard_map/convert_element_type | solution.py:110
  137.6 0.7 copy.19
  138.3 0.5 convert_element_type.19
  138.8 30.0 %all_to_all.70 = bf16[8,64,1024]{2,1,0:T(8,128)(2,1)S(1)} all-to-all(bf16[8,64,1024]{2,1,0:T(8,128)(2,1)S(1)} %convert_element_type.19), channel_id=1, replica_groups=mesh['head'=8,'kv'=4] {'head'}, dimensions={0} | all-to-all | bytes 2097152 | tf_op jit(solution)/shard_map/all_to_all | solution.py:111
  168.8 1.1 copy.25
  (30 shorter events, 0.3 us)
Async XLA Ops:
  0.0 0.9 copy-start
  1.6 13.1 %all-to-all-start.2 = ((bf16[64,8,128]{2,0,1:T(8,128)(2,1)}), bf16[64,8,128]{2,0,1:T(8,128)(2,1)S(1)}, u32[]{:S(2)}, u32[]{:S(2)}) async-start(bf16[64,8,128]{2,0,1:T(8,128)(2,1)} %copy_bitcast_fusion.1), calls=%async_computation.2 | async-start | bytes 262144 | tf_op jit(solution)/shard_map/all_to_all | solution.py:67
  14.7 10.1 %all-to-all-start = ((bf16[64,8,128]{2,0,1:T(8,128)(2,1)}), bf16[64,8,128]{2,0,1:T(8,128)(2,1)S(1)}, u32[]{:S(2)}, u32[]{:S(2)}) async-start(bf16[64,8,128]{2,0,1:T(8,128)(2,1)} %copy_bitcast_fusion.2), calls=%async_computation | async-start | bytes 262144 | tf_op jit(solution)/shard_map/all_to_all | solution.py:66
  18.1 10.3 %collective-permute-start = (bf16[512,128]{1,0:T(8,128)(2,1)S(1)}, bf16[512,128]{1,0:T(8,128)(2,1)S(1)}, u32[]{:S(2)}, u32[]{:S(2)}) collective-permute-start(bf16[512,128]{1,0:T(8,128)(2,1)S(1)} %bitcast.121), channel_id=1, source_target_pairs={{0,1},{1,2},{2,3},{3,0},{4,5},{5,6},{6,7},{7,4},{8,9},{9,10},{10,1... | collective-permute-start | bytes 393224 | tf_op jit(solution)/shard_map/ppermute | solution.py:88
  24.8 66.9 %all-to-all-start.1 = ((bf16[64,8,1024]{2,0,1:T(8,128)(2,1)}), bf16[64,8,1024]{2,0,1:T(8,128)(2,1)S(1)}, u32[]{:S(2)}, u32[]{:S(2)}) async-start(bf16[64,8,1024]{2,0,1:T(8,128)(2,1)} %bitcast.93), calls=%async_computation.1 | async-start | bytes 2097152 | tf_op jit(solution)/shard_map/all_to_all | solution.py:65
  28.3 49.9 %collective-permute-start.1 = (bf16[512,128]{1,0:T(8,128)(2,1)S(1)}, bf16[512,128]{1,0:T(8,128)(2,1)S(1)}, u32[]{:S(2)}, u32[]{:S(2)}) collective-permute-start(bf16[512,128]{1,0:T(8,128)(2,1)S(1)} %collective-permute-done), channel_id=1, source_target_pairs={{0,1},{1,2},{2,3},{3,0},{4,5},{5,6},{6,7},{7,4},{8,9},{9,10},{10,1... | collective-permute-start | bytes 393224 | tf_op jit(solution)/shard_map/ppermute | solution.py:88
  78.3 13.1 %collective-permute-start.2 = (bf16[512,128]{1,0:T(8,128)(2,1)S(1)}, bf16[512,128]{1,0:T(8,128)(2,1)S(1)}, u32[]{:S(2)}, u32[]{:S(2)}) collective-permute-start(bf16[512,128]{1,0:T(8,128)(2,1)S(1)} %collective-permute-done.1), channel_id=1, source_target_pairs={{0,1},{1,2},{2,3},{3,0},{4,5},{5,6},{6,7},{7,4},{8,9},{9,10},{10,1... | collective-permute-start | bytes 393224 | tf_op jit(solution)/shard_map/ppermute | solution.py:88
  102.2 4.1 %copy-start.1 = (f32[1,8,512,128]{3,2,1,0:T(8,128)S(1)}, f32[1,8,512,128]{3,2,1,0:T(8,128)}, u32[]{:S(2)}) copy-start(f32[1,8,512,128]{3,2,1,0:T(8,128)} %get-tuple-element.355) | copy-start | bytes 6291460 | tf_op jit(solution)/shard_map/while
  112.6 1.3 copy-start.2
  124.0 4.1 %copy-start.1 = (f32[1,8,512,128]{3,2,1,0:T(8,128)S(1)}, f32[1,8,512,128]{3,2,1,0:T(8,128)}, u32[]{:S(2)}) copy-start(f32[1,8,512,128]{3,2,1,0:T(8,128)} %get-tuple-element.355) | copy-start | bytes 6291460 | tf_op jit(solution)/shard_map/while
  134.3 1.3 copy-start.2
